TPU v7x, 256 devices: a whole 4x4x8 slice. The times are simulated.
256 devices in a mesh: pp: 4 (over x_hi, core), tp: 16 (over z, x_lo), dp: 4 (over y).
Axes of the slice: x: 4 (x_hi: 2, x_lo: 2; x = x_hi * 2 + x_lo), y: 4, z: 8, core: 2. Of those that a mesh axis runs over, the one named last changes fastest.
Arguments:
- layer_input: bfloat16 [4, 4, 128, 4096], P('pp', 'dp', 'tp'), may hold values from -4 to 4
- gate_pre: bfloat16 [4, 4, 128, 14784], P('pp', 'dp', None, 'tp'), may hold values from -8 to 8
- up_pre: bfloat16 [4, 4, 128, 14784], P('pp', 'dp', None, 'tp'), may hold values from -6 to 6
- hidden_grad: bfloat16 [4, 4, 128, 14784], P('pp', 'dp', None, 'tp'), may hold values from -0.59765625 to 0.59765625
- gate_weight: bfloat16 [4, 4096, 14784], P('pp', 'dp', 'tp'), may hold values from -0.09375 to 0.09375
Outputs:
- passed_grad: bfloat16 [4, 4, 128, 4096], P('pp', 'dp', 'tp')
- gate_weight_grad: bfloat16 [4, 4096, 14784], P('pp', 'dp', 'tp')
All inputs are finite; a program needn't handle non-finite values.
Results may differ from a plain program's by a relative error of at most 0.018.
Values may be sent and summed in bfloat16 or wider, within the bound.
A program may use at most 64 MiB of HBM per device.

v0:
```python
import jax
import jax.numpy as jnp
from jax import lax
from jax.sharding import PartitionSpec as P


def cut_along(x, dim, peers):
    before, after = (x.shape[:dim], x.shape[dim + 1 :])
    return jnp.moveaxis(x.reshape(*before, peers, -1, *after), dim, 0)


def sent_and_summed(x, axis, dim):
    tiles = cut_along(x, dim, lax.axis_size(axis))
    arrived = lax.all_to_all(tiles, axis, split_axis=0, concat_axis=0, tiled=True)
    return arrived.astype(jnp.float32).sum(axis=0)


def from_everyone(x, axis):
    copies = jnp.broadcast_to(x, (lax.axis_size(axis), *x.shape))
    return lax.all_to_all(copies, axis, split_axis=0, concat_axis=0, tiled=True)


def laid_out(tiles, dim):
    tiles = jnp.moveaxis(tiles, 0, dim)
    lengths = tiles.shape
    return tiles.reshape(*lengths[:dim], lengths[dim] * lengths[dim + 1], *lengths[dim + 2 :])


def collect(x, axis, dim):
    tiles = from_everyone(x, axis)
    return laid_out(tiles, dim)


def from_behind(block, axis, distance):
    devices = range(lax.axis_size(axis))
    route = [(i - distance, i) for i in devices if i - distance in devices]
    return lax.ppermute(block, axis, route)


def finish(partial_value):
    return sent_and_summed(partial_value.astype(jnp.bfloat16), "tp", 0).astype(jnp.bfloat16)


def on_device(layer_input, gate_pre, up_pre, hidden_grad, gate_weight):
    tokens_in = layer_input[0, 0]
    gate_val = gate_pre[0, 0].astype(jnp.float32)
    up_val = up_pre[0, 0].astype(jnp.float32)
    hidden_val = hidden_grad[0, 0].astype(jnp.float32)
    gate_local = gate_weight[0]
    rows_total = gate_val.shape[0]
    groups = lax.axis_size("dp")
    logistic = jax.nn.sigmoid(gate_val)
    gate_grad = (hidden_val * up_val * logistic * (1.0 + gate_val * (1.0 - logistic))).astype(
        jnp.bfloat16
    )
    gathered_in = collect(tokens_in, "tp", 0)
    contract_cols = (((1,), (1,)), ((), ()))
    all_grads = collect(gate_grad, "dp", 0)
    partial_value = lax.dot_general(
        all_grads, gate_local, contract_cols, preferred_element_type=jnp.float32
    )
    returned = lax.all_to_all(
        partial_value.astype(jnp.bfloat16), "dp", split_axis=0, concat_axis=1, tiled=True
    ).astype(partial_value.dtype)
    input_grad = finish(returned)
    in_columns = lax.all_to_all(gathered_in, "dp", split_axis=1, concat_axis=0, tiled=True)
    products = lax.dot_general(
        in_columns.reshape(groups, rows_total, in_columns.shape[1]),
        all_grads.reshape(groups, rows_total, all_grads.shape[1]),
        (((1,), (1,)), ((0,), (0,))),
        preferred_element_type=jnp.float32,
    )
    rounded = lax.optimization_barrier(products.astype(jnp.bfloat16))
    grads_total = jnp.sum(rounded.astype(jnp.float32), axis=0)
    passed = from_behind(input_grad, "pp", -1)
    gate_out = grads_total.astype(jnp.bfloat16)
    return (passed[None, None], gate_out[None])


def solution(mesh):
    return jax.shard_map(
        on_device,
        mesh=mesh,
        in_specs=(
            P("pp", "dp", "tp", None),
            P("pp", "dp", None, "tp"),
            P("pp", "dp", None, "tp"),
            P("pp", "dp", None, "tp"),
            P("pp", "dp", "tp"),
        ),
        out_specs=(P("pp", "dp", "tp", None), P("pp", "dp", "tp")),
        check_vma=False,
    )
```

profile of v0, /device:TPU:96, one launch (start us, length us, event | category | flops | bytes accessed | tf_op | source)
XLA Modules:
  0.0 136.5 jit_solution(6257464139573123061)
XLA Ops:
  0.6 0.0 copy-start
  0.6 1.5 %fusion.11 = bf16[128,924]{0,1:T(8,128)(2,1)S(1)} fusion(bf16[1,1,128,924]{2,3,1,0:T(8,128)(2,1)} %param.7, bf16[1,1,128,924]{2,3,1,0:T(8,128)(2,1)} %param.8, bf16[1,1,128,924]{2,3,1,0:T(8,128)(2,1)} %param.6), kind=kLoop, calls=%fused_computation.13 | loop fusion | flops 1537536 | bytes 946176 | tf_op jit(solution)/shard_map/convert_element_type | solution.py:53
  2.2 0.1 broadcast_in_dim.12
  2.3 18.3 %all_to_all.47 = bf16[4,128,924]{1,2,0:T(8,128)(2,1)S(1)} all-to-all(bf16[4,128,924]{1,2,0:T(8,128)(2,1)S(1)} %broadcast_in_dim.12), channel_id=1, replica_groups=mesh['pp'=4,'tp'=16,'dp'=4] {'dp'}, dimensions={0} | all-to-all | bytes 1892352 | tf_op jit(solution)/shard_map/all_to_all | solution.py:20
  20.6 0.5 copy.15
  21.1 0.4 pad
  21.5 0.2 copy.13
  21.7 0.0 copy-done
  21.7 1.3 fusion.2
  23.0 0.0 copy-start.1
  23.0 17.2 %all_to_all.48 = bf16[4,128,1024]{2,1,0:T(8,128)(2,1)} all-to-all(bf16[4,128,1024]{2,1,0:T(8,128)(2,1)S(1)} %bitcast.35), channel_id=1, replica_groups=mesh['pp'=4,'tp'=16,'dp'=4] {'dp'}, dimensions={0} | all-to-all | bytes 2097152 | tf_op jit(solution)/shard_map/all_to_all | solution.py:62
  40.2 0.0 copy-done.1
  40.2 1.1 broadcast_in_dim.14
  41.3 8.6 %all-to-all-start.3 = ((bf16[16,8,4096]{2,1,0:T(8,128)(2,1)}), bf16[16,8,4096]{2,1,0:T(8,128)(2,1)}, u32[]{:S(2)}, u32[]{:S(2)}) async-start(bf16[16,8,4096]{2,1,0:T(8,128)(2,1)} %broadcast_in_dim.14), calls=%async_computation.3 | async-start | bytes 2097152 | tf_op jit(solution)/shard_map/all_to_all | solution.py:20
  49.9 3.0 %copy.11 = bf16[128,4,1024]{2,1,0:T(4,128)(2,1)} copy(bf16[128,4,1024]{2,0,1:T(8,128)(2,1)} %bitcast.31) | data formatting | bytes 2097152 | tf_op jit(solution)/shard_map/all_to_all | solution.py:62
  52.9 2.6 %reshape.27 = bf16[16,8,4096]{2,1,0:T(8,128)(2,1)} reshape(bf16[128,4,1024]{2,1,0:T(4,128)(2,1)} %copy.11) | data formatting | bytes 2097152 | tf_op jit(solution)/shard_map/reshape | solution.py:9
  55.5 18.3 %all-to-all-done.3 = bf16[16,8,4096]{2,1,0:T(8,128)(2,1)} async-done(((bf16[16,8,4096]{2,1,0:T(8,128)(2,1)}), bf16[16,8,4096]{2,1,0:T(8,128)(2,1)}, u32[]{:S(2)}, u32[]{:S(2)}) %all-to-all-start.3) | async-done | bytes 1048608 | tf_op jit(solution)/shard_map/all_to_all | solution.py:20
  73.8 6.0 %all-to-all-start.2 = ((bf16[16,8,4096]{2,1,0:T(8,128)(2,1)}), bf16[16,8,4096]{2,1,0:T(8,128)(2,1)}, u32[]{:S(2)}, u32[]{:S(2)}) async-start(bf16[16,8,4096]{2,1,0:T(8,128)(2,1)} %reshape.27), calls=%async_computation.2 | async-start | bytes 2097152 | tf_op jit(solution)/shard_map/all_to_all | solution.py:14
  79.8 2.6 %all_to_all.39 = bf16[128,4,1024]{2,1,0:T(4,128)(2,1)} reshape(bf16[16,8,4096]{2,1,0:T(8,128)(2,1)} %all-to-all-done.3) | data formatting | bytes 2097152 | tf_op jit(solution)/shard_map/all_to_all | solution.py:66
  82.4 2.6 %copy.12 = bf16[128,4,1024]{2,0,1:T(8,128)(2,1)} copy(bf16[128,4,1024]{2,1,0:T(4,128)(2,1)} %all_to_all.39) | data formatting | bytes 2097152 | tf_op jit(solution)/shard_map/all_to_all | solution.py:66
  85.0 19.1 %all-to-all-done.2 = bf16[16,8,4096]{2,1,0:T(8,128)(2,1)} async-done(((bf16[16,8,4096]{2,1,0:T(8,128)(2,1)}), bf16[16,8,4096]{2,1,0:T(8,128)(2,1)}, u32[]{:S(2)}, u32[]{:S(2)}) %all-to-all-start.2) | async-done | bytes 1048608 | tf_op jit(solution)/shard_map/all_to_all | solution.py:14
  104.1 4.2 %all-to-all-start.4 = ((bf16[128,4,1024]{2,0,1:T(8,128)(2,1)}), bf16[128,4,1024]{2,0,1:T(8,128)(2,1)}, u32[]{:S(2)}, u32[]{:S(2)}) async-start(bf16[128,4,1024]{2,0,1:T(8,128)(2,1)} %copy.12), calls=%async_computation.4 | async-start | bytes 2097152 | tf_op jit(solution)/shard_map/all_to_all | solution.py:66
  108.3 1.4 %reduce_sum.24 = bf16[8,4096]{1,0:T(8,128)(2,1)S(1)} reduce(bf16[16,8,4096]{2,1,0:T(8,128)(2,1)} %all-to-all-done.2, bf16[]{:T(256)} %constant.5.clone.1), dimensions={0}, to_apply=%region_0.0 | reduce | flops 491520 | bytes 1114114 | tf_op jit(solution)/shard_map/reduce_sum | solution.py:15
  109.7 1.3 collective-permute-start
  111.0 11.7 %all-to-all-done.4 = bf16[128,4,1024]{2,0,1:T(8,128)(2,1)} async-done(((bf16[128,4,1024]{2,0,1:T(8,128)(2,1)}), bf16[128,4,1024]{2,0,1:T(8,128)(2,1)}, u32[]{:S(2)}, u32[]{:S(2)}) %all-to-all-start.4) | async-done | bytes 1048608 | tf_op jit(solution)/shard_map/all_to_all | solution.py:66
  122.6 6.4 %convert_bitcast_fusion = bf16[4,1024,924]{1,2,0:T(8,128)(2,1)} fusion(bf16[4,128,924]{1,2,0:T(8,128)(2,1)S(1)} %all_to_all.47, bf16[128,4,1024]{2,0,1:T(8,128)(2,1)} %all-to-all-done.4), kind=kOutput, calls=%fused_computation | convolution fusion | flops 972668928 | bytes 9564160 | tf_op jit(solution)/shard_map/dot_general | solution.py:67
  129.0 6.9 %reduce_sum.25 = bf16[1024,924]{0,1:T(8,128)(2,1)} reduce(bf16[4,1024,924]{1,2,0:T(8,128)(2,1)} %convert_bitcast_fusion, bf16[]{:T(256)} %constant.5.clone.1), dimensions={0}, to_apply=%region_1.0 | reduce | flops 2838528 | bytes 9461762 | tf_op jit(solution)/shard_map/reduce_sum | solution.py:74
  135.9 0.0 collective-permute-done
  135.9 0.6 copy.17
Async XLA Ops:
  0.6 21.0 %copy-start = (bf16[1,1024,924]{1,2,0:T(8,128)(2,1)S(1)}, bf16[1,1024,924]{1,2,0:T(8,128)(2,1)}, u32[]{:S(2)}) copy-start(bf16[1,1024,924]{1,2,0:T(8,128)(2,1)} %param.9) | copy-start | bytes 5677060
  23.0 17.3 %copy-start.1 = (bf16[1,1,8,4096]{3,2,1,0:T(8,128)(2,1)S(1)}, bf16[1,1,8,4096]{3,2,1,0:T(8,128)(2,1)}, u32[]{:S(2)}) copy-start(bf16[1,1,8,4096]{3,2,1,0:T(8,128)(2,1)} %param.5) | copy-start | bytes 196612
  41.3 32.5 %all-to-all-start.3 = ((bf16[16,8,4096]{2,1,0:T(8,128)(2,1)}), bf16[16,8,4096]{2,1,0:T(8,128)(2,1)}, u32[]{:S(2)}, u32[]{:S(2)}) async-start(bf16[16,8,4096]{2,1,0:T(8,128)(2,1)} %broadcast_in_dim.14), calls=%async_computation.3 | async-start | bytes 2097152 | tf_op jit(solution)/shard_map/all_to_all | solution.py:20
  73.8 30.3 %all-to-all-start.2 = ((bf16[16,8,4096]{2,1,0:T(8,128)(2,1)}), bf16[16,8,4096]{2,1,0:T(8,128)(2,1)}, u32[]{:S(2)}, u32[]{:S(2)}) async-start(bf16[16,8,4096]{2,1,0:T(8,128)(2,1)} %reshape.27), calls=%async_computation.2 | async-start | bytes 2097152 | tf_op jit(solution)/shard_map/all_to_all | solution.py:14
  104.1 18.6 %all-to-all-start.4 = ((bf16[128,4,1024]{2,0,1:T(8,128)(2,1)}), bf16[128,4,1024]{2,0,1:T(8,128)(2,1)}, u32[]{:S(2)}, u32[]{:S(2)}) async-start(bf16[128,4,1024]{2,0,1:T(8,128)(2,1)} %copy.12), calls=%async_computation.4 | async-start | bytes 2097152 | tf_op jit(solution)/shard_map/all_to_all | solution.py:66
  109.7 26.2 %collective-permute-start = (bf16[8,4096]{1,0:T(8,128)(2,1)S(1)}, bf16[8,4096]{1,0:T(8,128)(2,1)S(1)}, u32[]{:S(2)}, u32[]{:S(2)}) collective-permute-start(bf16[8,4096]{1,0:T(8,128)(2,1)S(1)} %reduce_sum.24), channel_id=1, source_target_pairs={{64,0},{128,64},{192,128},{65,1},{129,65},{193,129},{66,2},{130,66... | collective-permute-start | bytes 196616 | tf_op jit(solution)/shard_map/ppermute | solution.py:37
where the time goes:
time: 137 us
  waiting for transfers between devices  49 us (36%)
  blocking collectives  35.5 us (26%)
  starting transfers between devices  20.1 us (15%)
  local copies, waits for them, and re-layouts  13.7 us (10%)
  other arithmetic  9.78 us (7%)
  matrix products  7.67 us (6%)
    all_to_all x1, waiting for transfers between devices, sent_and_summed(): lax.all_to_all(tiles, axis, split_axis=0, concat_axis=0, tiled=True)  19.1 us
    all_to_all x1, blocking collectives, from_everyone(): return lax.all_to_all(copies, axis, split_axis=0, concat_axis=0, tiled=True)  18.3 us
    all_to_all x1, waiting for transfers between devices, from_everyone(): return lax.all_to_all(copies, axis, split_axis=0, concat_axis=0, tiled=True)  18.3 us
    all_to_all x1, blocking collectives, on_device(): lax.all_to_all(partial_value.astype(jnp.bfloat16), 'dp', split_axis=0, co...  17.2 us
    all_to_all x1, waiting for transfers between devices, on_device(): lax.all_to_all(gathered_in, 'dp', split_axis=1, concat_axis=0, tiled=True)  11.7 us
    all_to_all x1, starting transfers between devices, from_everyone(): return lax.all_to_all(copies, axis, split_axis=0, concat_axis=0, tiled=True)  8.6 us
    reduce_sum x1, other arithmetic, on_device(): grads_total = jnp.sum(rounded.astype(jnp.float32), axis=0)  6.88 us
    dot_general x1, matrix products, on_device(): lax.dot_general(in_columns.reshape(groups, rows_total, in_columns.shape[1...  6.38 us
  transfers between devices with their start and end apart: 4, of which 3 were waited for; matrix products, arithmetic and copies ran while one was open for 17% of the time, Pallas kernels for 0%

commit v1 on v0

--- a/solution.py
+++ b/solution.py
@@ -2,6 +2,21 @@
 import jax.numpy as jnp
 from jax import lax
 from jax.sharding import PartitionSpec as P
+
+
+def put_things(base_x, axis_k, vals):
+    z2 = base_x.shape
+    return jnp.moveaxis(
+        base_x.reshape(*z2[:axis_k], vals, z2[axis_k] // vals, *z2[axis_k + 1 :]), axis_k, 0
+    )
+
+
+def write_works(point, pos_dim):
+    point = jnp.moveaxis(point, 0, pos_dim)
+    taken_in = point.shape
+    return point.reshape(
+        *taken_in[:pos_dim], taken_in[pos_dim] * taken_in[pos_dim + 1], *taken_in[pos_dim + 2 :]
+    )
 
 
 def cut_along(x, dim, peers):
@@ -59,9 +74,25 @@
     partial_value = lax.dot_general(
         all_grads, gate_local, contract_cols, preferred_element_type=jnp.float32
     )
-    returned = lax.all_to_all(
-        partial_value.astype(jnp.bfloat16), "dp", split_axis=0, concat_axis=1, tiled=True
-    ).astype(partial_value.dtype)
+
+    def move_tasks(local_block, dev_axis, target, field_in):
+        local_next = lax.axis_size(dev_axis)
+        response = lax.axis_index(dev_axis)
+        local_out, val2 = (local_next, response)
+        front = put_things(local_block, target, local_out)
+        series = [front[val2]]
+        for it in [*range(1, local_out)]:
+            state_now = front[(val2 + it) % local_out]
+            outer = lax.ppermute(
+                state_now, dev_axis, perm=[(k, (k + it) % local_out) for k in range(local_out)]
+            )
+            series.append(outer)
+        front = jnp.stack(series, axis=0)[(val2 - jnp.arange(local_out)) % local_out]
+        return write_works(front, field_in)
+
+    returned = move_tasks(partial_value.astype(jnp.bfloat16), "dp", 0, 1).astype(
+        partial_value.dtype
+    )
     input_grad = finish(returned)
     in_columns = lax.all_to_all(gathered_in, "dp", split_axis=1, concat_axis=0, tiled=True)
     products = lax.dot_general(

time: 137 us -> 125 us (0.912)
  blocking collectives: 35.5 us -> 18.3 us
  starting transfers between devices: 20.1 us -> 25.1 us
  waiting for transfers between devices: 49 us -> 44.7 us
  local copies, waits for them, and re-layouts: 13.7 us -> 16.6 us
    all_to_all x1, waiting for transfers between devices: 18.3 us -> 0.01 us  [from_everyone(): return lax.all_to_all(copies, axis, split_axis=0, concat_axis=0, tiled=True)]
    all_to_all x1 -> x0, blocking collectives: 17.2 us -> none  [on_device(): lax.all_to_all(partial_value.astype(jnp.bfloat16), 'dp', split_axis=0, co...]
    ppermute x0 -> x3, waiting for transfers between devices: none -> 11.4 us  [move_tasks(): lax.ppermute(state_now, dev_axis, perm=[(k, (k + it) % local_out) for k i...]
    all_to_all x1 -> x0, local copies, waits for them, and re-layouts: 3 us -> none  [on_device(): lax.all_to_all(partial_value.astype(jnp.bfloat16), 'dp', split_axis=0, co...]
    transpose x0 -> x1, local copies, waits for them, and re-layouts: none -> 3 us  [write_works(): point = jnp.moveaxis(point, 0, pos_dim)]
    gather x0 -> x1, local copies, waits for them, and re-layouts: none -> 2.82 us  [move_tasks(): jnp.stack(series, axis=0)[(val2 - jnp.arange(local_out)) % local_out]]
    ppermute x0 -> x3, starting transfers between devices: none -> 2.71 us  [move_tasks(): lax.ppermute(state_now, dev_axis, perm=[(k, (k + it) % local_out) for k i...]
    all_to_all x1, starting transfers between devices: 5.99 us -> 8.13 us  [sent_and_summed(): lax.all_to_all(tiles, axis, split_axis=0, concat_axis=0, tiled=True)]
  transfers between devices with their start and end apart: 4 -> 7, of which waited for: 3 -> 5; matrix products, arithmetic and copies ran while one was open for 17% -> 23% of each run, Pallas kernels for 0% -> 0%
where the time goes in v1:
time: 125 us; the launch traced here: 124 us
  waiting for transfers between devices  44.7 us (36%)
  starting transfers between devices  25.1 us (20%)
  blocking collectives  18.3 us (15%)
  local copies, waits for them, and re-layouts  16.6 us (13%)
  other arithmetic  10.9 us (9%)
  matrix products  7.67 us (6%)
    all_to_all x1, waiting for transfers between devices, sent_and_summed(): lax.all_to_all(tiles, axis, split_axis=0, concat_axis=0, tiled=True)  20.5 us
    all_to_all x1, blocking collectives, from_everyone(): return lax.all_to_all(copies, axis, split_axis=0, concat_axis=0, tiled=True)  18.3 us
    all_to_all x1, waiting for transfers between devices, on_device(): lax.all_to_all(gathered_in, 'dp', split_axis=1, concat_axis=0, tiled=True)  12.8 us
    ppermute x3, waiting for transfers between devices, move_tasks(): lax.ppermute(state_now, dev_axis, perm=[(k, (k + it) % local_out) for k i...  11.4 us
    all_to_all x1, starting transfers between devices, from_everyone(): return lax.all_to_all(copies, axis, split_axis=0, concat_axis=0, tiled=True)  8.61 us
    all_to_all x1, starting transfers between devices, sent_and_summed(): lax.all_to_all(tiles, axis, split_axis=0, concat_axis=0, tiled=True)  8.13 us
    reduce_sum x1, other arithmetic, on_device(): grads_total = jnp.sum(rounded.astype(jnp.float32), axis=0)  6.88 us
    dot_general x1, matrix products, on_device(): lax.dot_general(in_columns.reshape(groups, rows_total, in_columns.shape[1...  6.37 us
  transfers between devices with their start and end apart: 7, of which 5 were waited for; matrix products, arithmetic and copies ran while one was open for 23% of the time, Pallas kernels for 0%

profile of v1, /device:TPU:96, one launch (start us, length us, event | category | flops | bytes accessed | tf_op | source)
XLA Modules:
  0.0 124.1 jit_solution(1561047385991948686)
XLA Ops:
  0.6 0.0 copy-start
  0.6 0.0 copy-start.1
  0.7 1.5 %fusion.11 = bf16[128,924]{0,1:T(8,128)(2,1)S(1)} fusion(bf16[1,1,128,924]{2,3,1,0:T(8,128)(2,1)} %param.7, bf16[1,1,128,924]{2,3,1,0:T(8,128)(2,1)} %param.8, bf16[1,1,128,924]{2,3,1,0:T(8,128)(2,1)} %param.6), kind=kLoop, calls=%fused_computation.15 | loop fusion | flops 1537536 | bytes 946176 | tf_op jit(solution)/shard_map/convert_element_type | solution.py:68
  2.2 0.1 broadcast_in_dim.13
  2.3 18.3 %all_to_all.31 = bf16[4,128,924]{1,2,0:T(8,128)(2,1)S(1)} all-to-all(bf16[4,128,924]{1,2,0:T(8,128)(2,1)S(1)} %broadcast_in_dim.13), channel_id=1, replica_groups=mesh['pp'=4,'tp'=16,'dp'=4] {'dp'}, dimensions={0} | all-to-all | bytes 1892352 | tf_op jit(solution)/shard_map/all_to_all | solution.py:35
  20.6 0.0 copy-done.1
  20.6 1.1 broadcast_in_dim.15
  21.8 8.6 %all-to-all-start.2 = ((bf16[16,8,4096]{2,1,0:T(8,128)(2,1)}), bf16[16,8,4096]{2,1,0:T(8,128)(2,1)}, u32[]{:S(2)}, u32[]{:S(2)}) async-start(bf16[16,8,4096]{2,1,0:T(8,128)(2,1)} %broadcast_in_dim.15), calls=%async_computation.2 | async-start | bytes 2097152 | tf_op jit(solution)/shard_map/all_to_all | solution.py:35
  30.4 0.5 copy.14
  30.9 0.4 pad.5
  31.3 0.2 copy.12
  31.4 0.0 copy-done
  31.4 1.3 %fusion.2 = bf16[512,1024]{1,0:T(8,128)(2,1)S(1)} fusion(bf16[512,924]{0,1:T(8,128)(2,1)S(1)} %bitcast.47, bf16[1,1024,924]{1,2,0:T(8,128)(2,1)S(1)} %copy-done), kind=kOutput, calls=%fused_computation.4 | convolution fusion | flops 969408512 | bytes 3887104 | tf_op jit(solution)/shard_map/dot_general | solution.py:74
  32.7 0.1 constant_dynamic-slice_fusion
  32.8 1.2 %collective-permute-start.2 = (bf16[128,1024]{1,0:T(8,128)(2,1)S(1)}, bf16[128,1024]{1,0:T(8,128)(2,1)S(1)}, u32[]{:S(2)}, u32[]{:S(2)}) collective-permute-start(bf16[128,1024]{1,0:T(8,128)(2,1)S(1)} %get-tuple-element.3), channel_id=1, source_target_pairs={{0,3},{1,0},{2,1},{3,2},{4,7},{5,4},{6,5},{7,6},{8,11},{9,8},{10,9... | collective-permute-start | bytes 786440 | tf_op jit(solution)/shard_map/ppermute | solution.py:86
  34.1 1.5 %collective-permute-start.1 = (bf16[128,1024]{1,0:T(8,128)(2,1)S(1)}, bf16[128,1024]{1,0:T(8,128)(2,1)S(1)}, u32[]{:S(2)}, u32[]{:S(2)}) collective-permute-start(bf16[128,1024]{1,0:T(8,128)(2,1)S(1)} %get-tuple-element.4), channel_id=1, source_target_pairs={{0,2},{1,3},{2,0},{3,1},{4,6},{5,7},{6,4},{7,5},{8,10},{9,11},{10,... | collective-permute-start | bytes 786440 | tf_op jit(solution)/shard_map/ppermute | solution.py:86
  35.5 0.0 collective-permute-start
  35.6 6.2 %collective-permute-done.2 = bf16[128,1024]{1,0:T(8,128)(2,1)S(1)} collective-permute-done((bf16[128,1024]{1,0:T(8,128)(2,1)S(1)}, bf16[128,1024]{1,0:T(8,128)(2,1)S(1)}, u32[]{:S(2)}, u32[]{:S(2)}) %collective-permute-start.2) | collective-permute-done | bytes 262176 | tf_op jit(solution)/shard_map/ppermute | solution.py:86
  41.8 2.4 %collective-permute-done.1 = bf16[128,1024]{1,0:T(8,128)(2,1)S(1)} collective-permute-done((bf16[128,1024]{1,0:T(8,128)(2,1)S(1)}, bf16[128,1024]{1,0:T(8,128)(2,1)S(1)}, u32[]{:S(2)}, u32[]{:S(2)}) %collective-permute-start.1) | collective-permute-done | bytes 262176 | tf_op jit(solution)/shard_map/ppermute | solution.py:86
  44.2 2.8 %collective-permute-done = bf16[128,1024]{1,0:T(8,128)(2,1)S(1)} collective-permute-done((bf16[128,1024]{1,0:T(8,128)(2,1)S(1)}, bf16[128,1024]{1,0:T(8,128)(2,1)S(1)}, u32[]{:S(2)}, u32[]{:S(2)}) %collective-permute-start) | collective-permute-done | bytes 262176 | tf_op jit(solution)/shard_map/ppermute | solution.py:86
  47.0 1.1 pad_maximum_fusion
  48.1 2.8 %gather_fusion = bf16[4,128,1024]{2,1,0:T(8,128)(2,1)} fusion(bf16[4,128,1024]{2,1,0:T(8,128)(2,1)} %pad_maximum_fusion, s32[1024]{0:T(1024)S(1)} %pad_clamp_fusion), kind=kCustom, calls=%fused_computation | custom fusion | bytes 2097168 | tf_op jit(solution)/shard_map/gather | solution.py:90
  50.9 3.0 %copy.10 = bf16[128,4,1024]{2,1,0:T(4,128)(2,1)} copy(bf16[128,4,1024]{2,0,1:T(8,128)(2,1)} %bitcast.42) | data formatting | bytes 2097152 | tf_op jit(solution)/shard_map/transpose | solution.py:15
  53.9 2.6 %reshape.78 = bf16[16,8,4096]{2,1,0:T(8,128)(2,1)} reshape(bf16[128,4,1024]{2,1,0:T(4,128)(2,1)} %copy.10) | data formatting | bytes 2097152 | tf_op jit(solution)/shard_map/reshape | solution.py:24
  56.5 0.0 all-to-all-done.2
  56.5 8.1 %all-to-all-start.1 = ((bf16[16,8,4096]{2,1,0:T(8,128)(2,1)}), bf16[16,8,4096]{2,1,0:T(8,128)(2,1)}, u32[]{:S(2)}, u32[]{:S(2)}) async-start(bf16[16,8,4096]{2,1,0:T(8,128)(2,1)} %reshape.78), calls=%async_computation.1 | async-start | bytes 2097152 | tf_op jit(solution)/shard_map/all_to_all | solution.py:29
  64.6 2.6 %all_to_all.24 = bf16[128,4,1024]{2,1,0:T(4,128)(2,1)} reshape(bf16[16,8,4096]{2,1,0:T(8,128)(2,1)} %all-to-all-done.2) | data formatting | bytes 2097152 | tf_op jit(solution)/shard_map/all_to_all | solution.py:97
  67.3 2.5 %copy.11 = bf16[128,4,1024]{2,0,1:T(8,128)(2,1)} copy(bf16[128,4,1024]{2,1,0:T(4,128)(2,1)} %all_to_all.24) | data formatting | bytes 2097152 | tf_op jit(solution)/shard_map/all_to_all | solution.py:97
  69.8 20.5 %all-to-all-done.1 = bf16[16,8,4096]{2,1,0:T(8,128)(2,1)} async-done(((bf16[16,8,4096]{2,1,0:T(8,128)(2,1)}), bf16[16,8,4096]{2,1,0:T(8,128)(2,1)}, u32[]{:S(2)}, u32[]{:S(2)}) %all-to-all-start.1) | async-done | bytes 1048608 | tf_op jit(solution)/shard_map/all_to_all | solution.py:29
  90.3 4.2 %all-to-all-start.3 = ((bf16[128,4,1024]{2,0,1:T(8,128)(2,1)}), bf16[128,4,1024]{2,0,1:T(8,128)(2,1)}, u32[]{:S(2)}, u32[]{:S(2)}) async-start(bf16[128,4,1024]{2,0,1:T(8,128)(2,1)} %copy.11), calls=%async_computation.3 | async-start | bytes 2097152 | tf_op jit(solution)/shard_map/all_to_all | solution.py:97
  94.6 1.4 %reduce_sum.24 = bf16[8,4096]{1,0:T(8,128)(2,1)S(1)} reduce(bf16[16,8,4096]{2,1,0:T(8,128)(2,1)} %all-to-all-done.1, bf16[]{:T(256)} %constant.46.clone.1), dimensions={0}, to_apply=%region_0.1 | reduce | flops 491520 | bytes 1114114 | tf_op jit(solution)/shard_map/reduce_sum | solution.py:30
  95.9 1.5 %collective-permute-start.3 = (bf16[8,4096]{1,0:T(8,128)(2,1)S(1)}, bf16[8,4096]{1,0:T(8,128)(2,1)S(1)}, u32[]{:S(2)}, u32[]{:S(2)}) collective-permute-start(bf16[8,4096]{1,0:T(8,128)(2,1)S(1)} %reduce_sum.24), channel_id=1, source_target_pairs={{64,0},{128,64},{192,128},{65,1},{129,65},{193,129},{66,2},{130,66... | collective-permute-start | bytes 196616 | tf_op jit(solution)/shard_map/ppermute | solution.py:52
  97.4 12.8 %all-to-all-done.3 = bf16[128,4,1024]{2,0,1:T(8,128)(2,1)} async-done(((bf16[128,4,1024]{2,0,1:T(8,128)(2,1)}), bf16[128,4,1024]{2,0,1:T(8,128)(2,1)}, u32[]{:S(2)}, u32[]{:S(2)}) %all-to-all-start.3) | async-done | bytes 1048608 | tf_op jit(solution)/shard_map/all_to_all | solution.py:97
  110.2 6.4 %convert_bitcast_fusion = bf16[4,1024,924]{1,2,0:T(8,128)(2,1)} fusion(bf16[4,128,924]{1,2,0:T(8,128)(2,1)S(1)} %all_to_all.31, bf16[128,4,1024]{2,0,1:T(8,128)(2,1)} %all-to-all-done.3), kind=kOutput, calls=%fused_computation.1 | convolution fusion | flops 972668928 | bytes 9564160 | tf_op jit(solution)/shard_map/dot_general | solution.py:98
  116.5 6.9 %reduce_sum.25 = bf16[1024,924]{0,1:T(8,128)(2,1)} reduce(bf16[4,1024,924]{1,2,0:T(8,128)(2,1)} %convert_bitcast_fusion, bf16[]{:T(256)} %constant.46.clone.1), dimensions={0}, to_apply=%region_1.2 | reduce | flops 2838528 | bytes 9461762 | tf_op jit(solution)/shard_map/reduce_sum | solution.py:105
  123.4 0.0 collective-permute-done.3
  123.4 0.6 copy.16
  (2 shorter events, 0.0 us)
Async XLA Ops:
  0.6 30.8 %copy-start = (bf16[1,1024,924]{1,2,0:T(8,128)(2,1)S(1)}, bf16[1,1024,924]{1,2,0:T(8,128)(2,1)}, u32[]{:S(2)}) copy-start(bf16[1,1024,924]{1,2,0:T(8,128)(2,1)} %param.9) | copy-start | bytes 5677060
  0.6 20.0 %copy-start.1 = (bf16[1,1,8,4096]{3,2,1,0:T(8,128)(2,1)S(1)}, bf16[1,1,8,4096]{3,2,1,0:T(8,128)(2,1)}, u32[]{:S(2)}) copy-start(bf16[1,1,8,4096]{3,2,1,0:T(8,128)(2,1)} %param.5) | copy-start | bytes 196612
  21.8 34.7 %all-to-all-start.2 = ((bf16[16,8,4096]{2,1,0:T(8,128)(2,1)}), bf16[16,8,4096]{2,1,0:T(8,128)(2,1)}, u32[]{:S(2)}, u32[]{:S(2)}) async-start(bf16[16,8,4096]{2,1,0:T(8,128)(2,1)} %broadcast_in_dim.15), calls=%async_computation.2 | async-start | bytes 2097152 | tf_op jit(solution)/shard_map/all_to_all | solution.py:35
  32.8 8.9 %collective-permute-start.2 = (bf16[128,1024]{1,0:T(8,128)(2,1)S(1)}, bf16[128,1024]{1,0:T(8,128)(2,1)S(1)}, u32[]{:S(2)}, u32[]{:S(2)}) collective-permute-start(bf16[128,1024]{1,0:T(8,128)(2,1)S(1)} %get-tuple-element.3), channel_id=1, source_target_pairs={{0,3},{1,0},{2,1},{3,2},{4,7},{5,4},{6,5},{7,6},{8,11},{9,8},{10,9... | collective-permute-start | bytes 786440 | tf_op jit(solution)/shard_map/ppermute | solution.py:86
  34.1 10.1 %collective-permute-start.1 = (bf16[128,1024]{1,0:T(8,128)(2,1)S(1)}, bf16[128,1024]{1,0:T(8,128)(2,1)S(1)}, u32[]{:S(2)}, u32[]{:S(2)}) collective-permute-start(bf16[128,1024]{1,0:T(8,128)(2,1)S(1)} %get-tuple-element.4), channel_id=1, source_target_pairs={{0,2},{1,3},{2,0},{3,1},{4,6},{5,7},{6,4},{7,5},{8,10},{9,11},{10,... | collective-permute-start | bytes 786440 | tf_op jit(solution)/shard_map/ppermute | solution.py:86
  35.5 11.4 %collective-permute-start = (bf16[128,1024]{1,0:T(8,128)(2,1)S(1)}, bf16[128,1024]{1,0:T(8,128)(2,1)S(1)}, u32[]{:S(2)}, u32[]{:S(2)}) collective-permute-start(bf16[128,1024]{1,0:T(8,128)(2,1)S(1)} %get-tuple-element.5), channel_id=1, source_target_pairs={{0,1},{1,2},{2,3},{3,0},{4,5},{5,6},{6,7},{7,4},{8,9},{9,10},{10,1... | collective-permute-start | bytes 786440 | tf_op jit(solution)/shard_map/ppermute | solution.py:86
  56.5 33.8 %all-to-all-start.1 = ((bf16[16,8,4096]{2,1,0:T(8,128)(2,1)}), bf16[16,8,4096]{2,1,0:T(8,128)(2,1)}, u32[]{:S(2)}, u32[]{:S(2)}) async-start(bf16[16,8,4096]{2,1,0:T(8,128)(2,1)} %reshape.78), calls=%async_computation.1 | async-start | bytes 2097152 | tf_op jit(solution)/shard_map/all_to_all | solution.py:29
  90.3 19.8 %all-to-all-start.3 = ((bf16[128,4,1024]{2,0,1:T(8,128)(2,1)}), bf16[128,4,1024]{2,0,1:T(8,128)(2,1)}, u32[]{:S(2)}, u32[]{:S(2)}) async-start(bf16[128,4,1024]{2,0,1:T(8,128)(2,1)} %copy.11), calls=%async_computation.3 | async-start | bytes 2097152 | tf_op jit(solution)/shard_map/all_to_all | solution.py:97
  95.9 27.5 %collective-permute-start.3 = (bf16[8,4096]{1,0:T(8,128)(2,1)S(1)}, bf16[8,4096]{1,0:T(8,128)(2,1)S(1)}, u32[]{:S(2)}, u32[]{:S(2)}) collective-permute-start(bf16[8,4096]{1,0:T(8,128)(2,1)S(1)} %reduce_sum.24), channel_id=1, source_target_pairs={{64,0},{128,64},{192,128},{65,1},{129,65},{193,129},{66,2},{130,66... | collective-permute-start | bytes 196616 | tf_op jit(solution)/shard_map/ppermute | solution.py:52
